TPU v7x, 32 devices: a whole 2x2x4 slice. The times are simulated.
32 devices in a mesh: sp: 16 (over z, x, core), tp: 2 (over y).
Axes of the slice: x: 2, y: 2, z: 4, core: 2. Of those that a mesh axis runs over, the one named last changes fastest.
Arguments:
- activations: bfloat16 [2, 2048, 8192], P(None, 'sp', 'tp'), may hold values from -250 to 250
- norm_gain: bfloat16 [8192], P('tp'), may hold values from 0.5 to 1.5
- keep_bits: int32 [2, 2048, 1024], P(None, 'sp', 'tp'), may hold values from 0 to 255, as said below
- key_value_weight: bfloat16 [1024, 8192], P('sp', 'tp'), may hold values from -0.0625 to 0.0625
- queries: bfloat16 [2, 2048, 4096], P('tp', 'sp'), may hold values from -68 to 68
- segment: int32 [4096], replicated, may hold values from 0 to 15, never falling along the last dimension, each value on 1 to 512 neighbouring positions
- cotangent: bfloat16 [2, 2048, 4096], P('tp', 'sp'), may hold values from -12 to 12
Outputs:
- attended: bfloat16 [2, 2048, 4096], P('tp', 'sp')
- grad_queries: bfloat16 [2, 2048, 4096], P('tp', 'sp')
- grad_activations: bfloat16 [2, 2048, 8192], P(None, 'sp', 'tp')
- grad_weight: float32 [1024, 8192], P('sp', 'tp')
- grad_gain: float32 [8192], P('tp')
Inputs may be any that keep to these rules, and one draw needn't show every extreme that they name: Bit j of keep_bits[a, b, w] is the keep flag of feature 8 w + j. segment numbers never fall along the sequence; each document covers 1 to 512 positions, and one covers exactly 512.
All inputs are finite; a program needn't handle non-finite values.
Results may differ from a plain program's by a relative error of at most 0.012.
The roundings to bfloat16 on the way count: a program that leaves them out, or rounds other values in their place, can miss the bound.
Values may be sent and summed in bfloat16 or wider, within the bound.
A program may use at most 128 MiB of HBM per device.

v0:
```python
import jax
import jax.numpy as jnp
from jax import lax
from jax.sharding import PartitionSpec as P

D = 8192
HQ = 32
KVH = 4
HD = 128
DOC = 512
GROUP = 8
EPS = 1e-05
KEEP_RATE = 0.9
MASKED_SCORE = -1e30


def shifted(block, axis, distance):
    devices = range(lax.axis_size(axis))
    route = [(i - distance, i) for i in devices if i - distance in devices]
    return lax.ppermute(block, axis, route)


def unpack_flags(words):
    shifts = jnp.arange(8, dtype=jnp.int32)
    flags = jnp.bitwise_and(jnp.right_shift(words[..., None], shifts), 1)
    return flags.reshape(words.shape[:-1] + (words.shape[-1] * 8,)).astype(jnp.float32)


def group_sum(per_head, group_size):
    row_count, head_count, width = per_head.shape
    summed = jnp.sum(
        per_head.reshape(row_count, head_count // group_size, group_size, width), axis=2
    )
    return summed.reshape(row_count, head_count // group_size * width).astype(jnp.bfloat16)


def block_attention(query_block, pair_window, grad_block, allowed):
    score_scale = HD ** (-0.5)
    key_part = pair_window[:, :, :HD]
    value_part = pair_window[:, :, HD:]
    scores = (
        jnp.einsum("qhd,khd->hqk", query_block, key_part, preferred_element_type=jnp.float32)
        * score_scale
    )
    scores = jnp.where(allowed[None], scores, MASKED_SCORE)
    row_max = jnp.max(scores, axis=2, keepdims=True)
    weights = jnp.exp(scores - row_max)
    probabilities = weights / jnp.sum(weights, axis=2, keepdims=True)
    probs_low = probabilities.astype(jnp.bfloat16)
    attended = jnp.einsum(
        "hqk,khd->qhd", probs_low, value_part, preferred_element_type=jnp.float32
    ).astype(jnp.bfloat16)
    grad_probs = jnp.einsum(
        "qhd,khd->hqk", grad_block, value_part, preferred_element_type=jnp.float32
    )
    row_inner = jnp.sum(probabilities * grad_probs, axis=2, keepdims=True)
    grad_scores = (probabilities * (grad_probs - row_inner)).astype(jnp.bfloat16)
    grad_query = (
        jnp.einsum("hqk,khd->qhd", grad_scores, key_part, preferred_element_type=jnp.float32)
        * score_scale
    ).astype(jnp.bfloat16)
    grad_keys = (
        jnp.einsum("hqk,qhd->khd", grad_scores, query_block, preferred_element_type=jnp.float32)
        * score_scale
    )
    grad_values = jnp.einsum(
        "hqk,qhd->khd", probs_low, grad_block, preferred_element_type=jnp.float32
    )
    return (attended, grad_query, jnp.concatenate([grad_keys, grad_values], axis=2))


def run_blocks(query_rows, grad_rows, pair_rows, seg_query, seg_keys):
    block_count = query_rows.shape[0] // DOC
    head_count = query_rows.shape[1]
    causal = (
        jnp.arange(2 * DOC, dtype=jnp.int32)[None, :]
        <= jnp.arange(DOC, dtype=jnp.int32)[:, None] + DOC
    )

    def attend_step(pending, block_index):
        offset = block_index * DOC
        query_block = lax.dynamic_slice_in_dim(query_rows, offset, DOC, 0)
        grad_block = lax.dynamic_slice_in_dim(grad_rows, offset, DOC, 0)
        pair_window = lax.dynamic_slice_in_dim(pair_rows, offset, 2 * DOC, 0)
        block_segs = lax.dynamic_slice_in_dim(seg_query, offset, DOC, 0)
        window_segs = lax.dynamic_slice_in_dim(seg_keys, offset, 2 * DOC, 0)
        allowed = causal & (block_segs[:, None] == window_segs[None, :])
        attended, grad_query, grad_window = block_attention(
            query_block, pair_window, grad_block, allowed
        )
        return (grad_window[DOC:], (attended, grad_query, pending + grad_window[:DOC]))

    return lax.scan(
        attend_step,
        jnp.zeros((DOC, head_count, 2 * HD), jnp.float32),
        jnp.arange(block_count, dtype=jnp.int32),
    )


def on_device(activations, norm_gain, keep_bits, key_value_weight, queries, segment, cotangent):
    sp_size = lax.axis_size("sp")
    tp_size = lax.axis_size("tp")
    tp_index = lax.axis_index("tp")
    block_count, row_count, local_width = activations.shape
    seq_length = row_count * sp_size * tp_size
    query_span = row_count * sp_size
    heads_here = HQ // sp_size
    gain_wide = norm_gain.astype(jnp.float32)
    input_wide = activations.astype(jnp.float32)
    square_total = lax.psum(jnp.sum(input_wide * input_wide, axis=2), "tp")
    inv_rms = lax.rsqrt(square_total[..., None] / D + EPS)
    drop_scale = unpack_flags(keep_bits) / KEEP_RATE
    normed = (input_wide * inv_rms * gain_wide * drop_scale).astype(jnp.bfloat16)
    weight_full = lax.all_gather(key_value_weight, "sp", axis=0, tiled=True)
    pair_tokens = lax.psum_scatter(
        jnp.einsum("arf,cf->arc", normed, weight_full, preferred_element_type=jnp.float32),
        "tp",
        scatter_dimension=0,
        tiled=True,
    )[0].astype(jnp.bfloat16)
    pair_heads = pair_tokens.reshape(row_count, KVH, 2 * HD)
    query_tokens = queries[0].reshape(row_count, HQ, HD)
    grad_tokens = cotangent[0].reshape(row_count, HQ, HD)
    query_here = lax.all_to_all(query_tokens, "sp", split_axis=1, concat_axis=0, tiled=True)
    pair_every = lax.all_gather(pair_heads, "sp", axis=0, tiled=True)
    first_head = lax.axis_index("sp") * heads_here
    owner_head = (first_head + jnp.arange(heads_here, dtype=jnp.int32)) // GROUP
    selector = (owner_head[:, None] == jnp.arange(KVH, dtype=jnp.int32)[None, :]).astype(
        jnp.bfloat16
    )
    pair_here = jnp.einsum(
        "pgc,jg->pjc", pair_every, selector, preferred_element_type=jnp.float32
    ).astype(jnp.bfloat16)
    grad_here = lax.all_to_all(grad_tokens, "sp", split_axis=1, concat_axis=0, tiled=True)
    rim_pairs = shifted(pair_here[query_span - DOC :], "tp", 1)
    pair_extended = jnp.concatenate([rim_pairs, pair_here], axis=0)
    segment_padded = jnp.concatenate([jnp.full((DOC,), -1, jnp.int32), segment])
    segment_keys = lax.dynamic_slice_in_dim(
        segment_padded, tp_index * query_span, query_span + DOC, 0
    )
    segment_query = segment_keys[DOC:]
    final_tail, (outputs, query_grads, finished) = run_blocks(
        query_here, grad_here, pair_extended, segment_query, segment_keys
    )
    rim_back = shifted(finished[0], "tp", -1)
    tail_grad = final_tail + rim_back
    pair_grad_heads = jnp.concatenate(
        [finished[1:].reshape(query_span - DOC, heads_here, 2 * HD), tail_grad], axis=0
    ).astype(jnp.bfloat16)
    attended_heads = outputs.reshape(query_span, heads_here, HD)
    query_grad_heads = query_grads.reshape(query_span, heads_here, HD)
    attended_tokens, query_grad_tokens, pair_grad_tokens = (
        lax.all_to_all(attended_heads, "sp", split_axis=0, concat_axis=1, tiled=True),
        lax.all_to_all(query_grad_heads, "sp", split_axis=0, concat_axis=1, tiled=True),
        lax.all_to_all(pair_grad_heads, "sp", split_axis=0, concat_axis=1, tiled=True),
    )
    pair_grad_rows = group_sum(pair_grad_tokens.astype(jnp.float32), GROUP)
    pair_grad_all = lax.all_gather(pair_grad_rows[None], "tp", axis=0, tiled=True)
    hidden_grad = jnp.einsum(
        "arc,cf->arf", pair_grad_all, weight_full, preferred_element_type=jnp.float32
    )
    grad_weight = lax.psum_scatter(
        jnp.einsum("arc,arf->cf", pair_grad_all, normed, preferred_element_type=jnp.float32),
        "sp",
        scatter_dimension=0,
        tiled=True,
    ) * seq_length ** (-0.5)
    scaled = hidden_grad * drop_scale
    upstream = scaled * gain_wide
    row_dots = lax.psum(jnp.sum(upstream * input_wide, axis=2), "tp")[..., None]
    grad_activations = (
        inv_rms * upstream - input_wide * (inv_rms * inv_rms * inv_rms) * row_dots / D
    ).astype(jnp.bfloat16)
    gain_local = jnp.sum(scaled * input_wide * inv_rms, axis=(0, 1))
    grad_gain = lax.psum(gain_local, "sp") * seq_length ** (-0.5)
    attended = attended_tokens.reshape(1, row_count, HQ * HD)
    grad_queries = query_grad_tokens.reshape(1, row_count, HQ * HD)
    return (attended, grad_queries, grad_activations, grad_weight, grad_gain)


def solution(mesh):
    return jax.shard_map(
        on_device,
        mesh=mesh,
        in_specs=(
            P(None, "sp", "tp"),
            P("tp"),
            P(None, "sp", "tp"),
            P("sp", "tp"),
            P("tp", "sp", None),
            P(),
            P("tp", "sp", None),
        ),
        out_specs=(
            P("tp", "sp", None),
            P("tp", "sp", None),
            P(None, "sp", "tp"),
            P("sp", "tp"),
            P("tp"),
        ),
        check_vma=False,
    )
```

profile of v0, /device:TPU:0, one launch (start us, length us, event | category | flops | bytes accessed | tf_op | source)
XLA Modules:
  0.0 660.8 jit_solution(8027859273964167711)
XLA Ops:
  9.9 2.2 broadcast_bitcast_fusion
  12.1 5.8 copy.119
  18.6 5.9 psum.21
  25.1 4.7 fusion.44
  29.8 57.4 %all-gather.3.cloned.1.call-done = bf16[1024,4096]{1,0:T(8,128)(2,1)} async-done(((bf16[64,4096]{1,0:T(8,128)(2,1)}), bf16[1024,4096]{1,0:T(8,128)(2,1)}) %all-gather.3.cloned.1.call-update) | async-done | bytes 8388624 | tf_op jit(solution)/shard_map/all_gather | solution.py:114
  87.2 7.4 %fusion.36 = f32[2,128,1024]{2,1,0:T(8,128)} fusion(bf16[2,128,4096]{2,1,0:T(8,128)(2,1)} %fusion.44, bf16[1024,4096]{1,0:T(8,128)(2,1)} %all-gather.3.cloned.1.call-done), kind=kOutput, calls=%fused_computation.53 | convolution fusion | flops 2147483648 | bytes 11534336 | tf_op jit(solution)/shard_map/arf,cf->arc/dot_general | solution.py:116
  94.6 19.1 %reduce-scatter.3.cloned.1.call-done = f32[1,128,1024]{2,1,0:T(8,128)} async-done(((f32[2,128,1024]{2,1,0:T(8,128)}), f32[1,128,1024]{2,1,0:T(8,128)}) %reduce-scatter.3.cloned.1.call-update) | async-done | bytes 524304 | tf_op jit(solution)/shard_map/reduce_scatter | solution.py:115
  117.0 5.6 all-to-all-start.1
  123.9 30.0 %all-to-all-done.1 = bf16[128,32,128]{0,2,1:T(8,128)(2,1)S(1)} async-done(((bf16[128,32,128]{0,2,1:T(8,128)(2,1)}), bf16[128,32,128]{0,2,1:T(8,128)(2,1)S(1)}, u32[]{:S(2)}, u32[]{:S(2)}) %all-to-all-start.1) | async-done | bytes 1048608 | tf_op jit(solution)/shard_map/all_to_all | solution.py:134
  153.9 6.8 %all-to-all-start = ((bf16[128,32,128]{0,2,1:T(8,128)(2,1)}), bf16[128,32,128]{0,2,1:T(8,128)(2,1)S(1)}, u32[]{:S(2)}, u32[]{:S(2)}) async-start(bf16[128,32,128]{0,2,1:T(8,128)(2,1)} %bitcast), calls=%async_computation | async-start | bytes 2097152 | tf_op jit(solution)/shard_map/all_to_all | solution.py:124
  160.8 33.3 %all-gather.5.cloned.1.call-done = bf16[2048,4,256]{2,1,0:T(4,128)(2,1)} async-done(((bf16[128,4,256]{2,1,0:T(4,128)(2,1)}), bf16[2048,4,256]{2,1,0:T(4,128)(2,1)}) %all-gather.5.cloned.1.call-update) | async-done | bytes 4194320 | tf_op jit(solution)/shard_map/all_gather | solution.py:125
  194.1 4.6 fusion.52
  201.2 5.1 collective-permute-start
  208.4 8.4 %collective-permute-done = bf16[512,2,256]{2,1,0:T(2,128)(2,1)} collective-permute-done((bf16[512,2,256]{2,1,0:T(2,128)(2,1)}, bf16[512,2,256]{2,1,0:T(2,128)(2,1)}, u32[]{:S(2)}, u32[]{:S(2)}) %collective-permute-start) | collective-permute-done | bytes 524320 | tf_op jit(solution)/shard_map/ppermute | solution.py:20
  216.9 9.7 %pad_maximum_fusion.1 = bf16[2560,2,256]{2,1,0:T(2,128)(2,1)} fusion(bf16[2048,2,256]{2,1,0:T(2,128)(2,1)} %copy-done.10, bf16[512,2,256]{2,1,0:T(2,128)(2,1)} %collective-permute-done), kind=kLoop, calls=%fused_computation.77 | loop fusion | flops 1310720 | bytes 5242880 | tf_op jit(solution)/shard_map/concatenate | solution.py:136
  227.7 87.9 %while.17 = (s32[]{:T(128)}, f32[512,2,256]{0,2,1:T(8,128)}, bf16[4,512,2,128]{3,1,0,2:T(8,128)(2,1)}, bf16[4,512,2,128]{3,1,0,2:T(8,128)(2,1)}, f32[4,512,2,256...) while((s32[]{:T(128)}, f32[512,2,256]{0,2,1:T(8,128)}, ...), condition=%wide.region_7.8_spmd.clone, body=%wide.region_3.7_spmd.clone.sunk | while | flops 1631453184 | bytes 125355472 | solution.py:93
  232.4 2.0 fusion.95
  237.5 3.2 multiply_reduce_fusion.2
  243.6 2.0 fusion.96
  254.3 2.0 fusion.95
  259.5 3.2 multiply_reduce_fusion.2
  265.6 2.0 fusion.96
  276.3 2.0 fusion.95
  281.5 3.2 multiply_reduce_fusion.2
  298.3 2.0 fusion.95
  303.5 3.2 multiply_reduce_fusion.2
  315.6 5.3 copy.133
  320.8 2.4 slice_bitcast_fusion
  324.7 3.3 copy.132
  329.5 20.6 %collective-permute-done.1 = f32[512,2,256]{2,0,1:T(8,128)} collective-permute-done((f32[512,2,256]{2,0,1:T(8,128)}, f32[512,2,256]{2,0,1:T(8,128)}, u32[]{:S(2)}, u32[]{:S(2)}) %collective-permute-start.1) | collective-permute-done | bytes 1048608 | tf_op jit(solution)/shard_map/ppermute | solution.py:20
  351.8 12.8 %copy.135 = bf16[2048,2,256]{2,1,0:T(2,128)(2,1)S(1)} copy(bf16[2048,2,256]{2,0,1:T(8,128)(2,1)S(1)} %pad_maximum_fusion.2) | data formatting | bytes 4194304 | tf_op jit(solution)/shard_map/concatenate | solution.py:147
  364.7 50.7 %all_to_all.75 = bf16[2048,2,256]{2,1,0:T(2,128)(2,1)S(1)} all-to-all(bf16[2048,2,256]{2,1,0:T(2,128)(2,1)S(1)} %copy.135), channel_id=1, replica_groups=mesh['sp'=16,'tp'=2] {'sp'}, dimensions={0} | all-to-all | bytes 4194304 | tf_op jit(solution)/shard_map/all_to_all | solution.py:155
  415.4 12.2 %convert_reduce_fusion = f32[2048,256]{1,0:T(8,128)} fusion(bf16[2048,2,256]{2,1,0:T(2,128)(2,1)S(1)} %all_to_all.75), kind=kLoop, calls=%fused_computation.72 | loop fusion | flops 1572864 | bytes 4194304 | tf_op jit(solution)/shard_map/reduce_sum | solution.py:31
  429.7 9.8 %all_gather.11 = bf16[2,128,1024]{2,1,0:T(8,128)(2,1)S(1)} all-gather(bf16[1,128,1024]{2,1,0:T(8,128)(2,1)S(1)} %copy.137), channel_id=1, replica_groups=mesh['sp'=16,'tp'=2] {'tp'}, dimensions={0}, use_global_device_ids=true | all-gather | bytes 786432 | tf_op jit(solution)/shard_map/all_gather | solution.py:158
  440.4 8.1 %convolution_bitcast_fusion.1 = f32[1024,4096]{1,0:T(8,128)} fusion(bf16[2,128,1024]{2,1,0:T(8,128)(2,1)S(1)} %all_gather.11, bf16[2,128,4096]{2,1,0:T(8,128)(2,1)S(1)} %copy-done.9), kind=kOutput, calls=%fused_computation.50 | convolution fusion | flops 2147483648 | bytes 19398656 | tf_op jit(solution)/shard_map/arc,arf->cf/dot_general | solution.py:163
  449.7 9.4 %copy.125 = bf16[2048,2,128]{2,1,0:T(2,128)(2,1)} copy(bf16[2048,2,128]{2,0,1:T(8,128)(2,1)S(1)} %bitcast.97) | data formatting | bytes 2097152 | tf_op jit(solution)/shard_map/reshape | solution.py:150
  459.2 4.6 all-to-all-start.2
  463.7 9.5 %copy.129 = bf16[2048,2,128]{2,1,0:T(2,128)(2,1)} copy(bf16[2048,2,128]{2,0,1:T(8,128)(2,1)S(1)} %bitcast.98) | data formatting | bytes 2097152 | tf_op jit(solution)/shard_map/reshape | solution.py:151
  473.2 13.4 %all-to-all-done.2 = bf16[2048,2,128]{2,1,0:T(2,128)(2,1)S(1)} async-done(((bf16[2048,2,128]{2,1,0:T(2,128)(2,1)}), bf16[2048,2,128]{2,1,0:T(2,128)(2,1)S(1)}, u32[]{:S(2)}, u32[]{:S(2)}) %all-to-all-start.2) | async-done | bytes 1048608 | tf_op jit(solution)/shard_map/all_to_all | solution.py:153
  486.6 17.4 %all-to-all-start.3 = ((bf16[2048,2,128]{2,1,0:T(2,128)(2,1)}), bf16[2048,2,128]{2,1,0:T(2,128)(2,1)S(1)}, u32[]{:S(2)}, u32[]{:S(2)}) async-start(bf16[2048,2,128]{2,1,0:T(2,128)(2,1)} %copy.129), calls=%async_computation.4 | async-start | bytes 2097152 | tf_op jit(solution)/shard_map/all_to_all | solution.py:154
  505.5 2.4 copy.139
  508.0 34.9 %all-to-all-done.3 = bf16[2048,2,128]{2,1,0:T(2,128)(2,1)S(1)} async-done(((bf16[2048,2,128]{2,1,0:T(2,128)(2,1)}), bf16[2048,2,128]{2,1,0:T(2,128)(2,1)S(1)}, u32[]{:S(2)}, u32[]{:S(2)}) %all-to-all-start.3) | async-done | bytes 1048608 | tf_op jit(solution)/shard_map/all_to_all | solution.py:154
  547.0 10.3 %fusion.51 = (f32[4096]{0:T(1024)S(1)}, f32[2,128]{1,0:T(2,128)S(1)}, f32[2,128,4096]{2,1,0:T(8,128)}) fusion(bf16[2,128,4096]{2,1,0:T(8,128)(2,1)S(1)} %copy-done.6, f32[2,128]{1,0:T(2,128)S(1)} %copy-done.22, f32[4096]{0:T(1024)S(1)} %copy-done.17, s32[2,128,4096]{2,1,0:T(8,128)} %copy.119, s32[4096]{0:T(1024)S(1)} %copy-done.19, ...), kind=kOutput, calls=%fused_computation.71 | convolution fusion | flops 2160062208 | bytes 19449856 | tf_op jit(solution)/shard_map/arc,cf->arf/dot_general | solution.py:159
  557.3 4.9 psum.22
  562.2 72.5 %psum.23 = f32[4096]{0:T(1024)S(1)} all-reduce(f32[4096]{0:T(1024)S(1)} %get-tuple-element.193), channel_id=1, replica_groups=mesh['sp'=16,'tp'=2] {'sp'}, use_global_device_ids=true, to_apply=%region_14.15 | all-reduce | flops 4096 | bytes 32768 | tf_op jit(solution)/shard_map/psum | solution.py:175
  635.3 4.9 fusion.48
  640.2 11.6 %reduce-scatter.5.cloned.1.call-done = f32[64,4096]{1,0:T(8,128)} async-done(((f32[1024,4096]{1,0:T(8,128)}), f32[64,4096]{1,0:T(8,128)}) %reduce-scatter.5.cloned.1.call-update) | async-done | bytes 1048592 | tf_op jit(solution)/shard_map/reduce_scatter | solution.py:162
  651.8 2.3 broadcast_multiply_fusion
  (191 shorter events, 88.9 us)
Async XLA Ops:
  7.2 80.0 %all-gather.3.cloned.1.call-start = ((), (), s32[]{:S(2)}) async-start(), calls=%async_computation.7 | async-start | bytes 8912896 | tf_op jit(solution)/shard_map/all_gather | solution.py:114
  7.9 105.8 %reduce-scatter.3.cloned.1.call-start = ((), (), s32[]{:S(2)}) async-start(), calls=%async_computation.8 | async-start | bytes 1572864 | tf_op jit(solution)/shard_map/reduce_scatter | solution.py:115
  8.6 16.4 %copy-start.16 = (f32[4096]{0:T(1024)}, f32[4096]{0:T(1024)S(1)}, u32[]{:S(2)}) copy-start(f32[4096]{0:T(1024)S(1)} %convert_element_type.69) | copy-start | bytes 49156
  12.1 5.9 copy-start.5
  18.1 11.7 %copy-start.18 = (s32[4096]{0:T(1024)}, s32[4096]{0:T(1024)S(1)}, u32[]{:S(2)}) copy-start(s32[4096]{0:T(1024)S(1)} %shift_right_arithmetic.23) | copy-start | bytes 49156
  25.1 4.7 copy-start.21
  29.8 85.9 %copy-start.12 = (bf16[1,128,4096]{2,1,0:T(8,128)(2,1)S(1)}, bf16[1,128,4096]{2,1,0:T(8,128)(2,1)}, u32[]{:S(2)}) copy-start(bf16[1,128,4096]{2,1,0:T(8,128)(2,1)} %param.15) | copy-start | bytes 3145732
  94.5 28.1 %copy-start.13 = (bf16[1,128,4096]{2,1,0:T(8,128)(2,1)S(1)}, bf16[1,128,4096]{2,1,0:T(8,128)(2,1)}, u32[]{:S(2)}) copy-start(bf16[1,128,4096]{2,1,0:T(8,128)(2,1)} %param.13) | copy-start | bytes 3145732
  94.6 99.5 %all-gather.5.cloned.1.call-start = ((), (), s32[]{:S(2)}) async-start(), calls=%async_computation.9 | async-start | bytes 4456448 | tf_op jit(solution)/shard_map/all_gather | solution.py:125
  117.0 36.9 %all-to-all-start.1 = ((bf16[128,32,128]{0,2,1:T(8,128)(2,1)}), bf16[128,32,128]{0,2,1:T(8,128)(2,1)S(1)}, u32[]{:S(2)}, u32[]{:S(2)}) async-start(bf16[128,32,128]{0,2,1:T(8,128)(2,1)} %bitcast.9), calls=%async_computation.2 | async-start | bytes 2097152 | tf_op jit(solution)/shard_map/all_to_all | solution.py:134
  153.9 53.9 %all-to-all-start = ((bf16[128,32,128]{0,2,1:T(8,128)(2,1)}), bf16[128,32,128]{0,2,1:T(8,128)(2,1)S(1)}, u32[]{:S(2)}, u32[]{:S(2)}) async-start(bf16[128,32,128]{0,2,1:T(8,128)(2,1)} %bitcast), calls=%async_computation | async-start | bytes 2097152 | tf_op jit(solution)/shard_map/all_to_all | solution.py:124
  160.7 491.1 %reduce-scatter.5.cloned.1.call-start = ((), (), s32[]{:S(2)}) async-start(), calls=%async_computation.10 | async-start | bytes 17825792 | tf_op jit(solution)/shard_map/reduce_scatter | solution.py:162
  160.8 45.5 %copy-start.20 = (s32[4096]{0:T(1024)S(1)}, s32[4096]{0:T(1024)}, u32[]{:S(2)}) copy-start(s32[4096]{0:T(1024)} %param.14) | copy-start | bytes 49156
  201.2 15.7 %collective-permute-start = (bf16[512,2,256]{2,1,0:T(2,128)(2,1)}, bf16[512,2,256]{2,1,0:T(2,128)(2,1)}, u32[]{:S(2)}, u32[]{:S(2)}) collective-permute-start(bf16[512,2,256]{2,1,0:T(2,128)(2,1)} %slice.35), channel_id=1, source_target_pairs={{0,1},{2,3},{4,5},{6,7},{8,9},{10,11},{12,13},{14,15},{16,17},{18,... | collective-permute-start | bytes 1572872 | tf_op jit(solution)/shard_map/ppermute | solution.py:20
  227.7 6.7 %copy-start.7 = (bf16[2048,2,128]{2,0,1:T(8,128)(2,1)}, bf16[2048,2,128]{2,0,1:T(8,128)(2,1)S(1)}, u32[]{:S(2)}) copy-start(bf16[2048,2,128]{2,0,1:T(8,128)(2,1)S(1)} %get-tuple-element.361) | copy-start | bytes 3145732 | tf_op jit(solution)/shard_map/while
  234.4 2.0 copy-start
  237.5 3.5 copy-start.1
  242.7 2.9 copy-start.2
  245.7 1.7 copy-start.3
  247.4 2.3 copy-start.8
  249.6 6.7 %copy-start.7 = (bf16[2048,2,128]{2,0,1:T(8,128)(2,1)}, bf16[2048,2,128]{2,0,1:T(8,128)(2,1)S(1)}, u32[]{:S(2)}) copy-start(bf16[2048,2,128]{2,0,1:T(8,128)(2,1)S(1)} %get-tuple-element.361) | copy-start | bytes 3145732 | tf_op jit(solution)/shard_map/while
  256.4 2.0 copy-start
  259.5 3.5 copy-start.1
  264.7 2.9 copy-start.2
  267.6 1.7 copy-start.3
  269.3 2.3 copy-start.8
  271.6 6.7 %copy-start.7 = (bf16[2048,2,128]{2,0,1:T(8,128)(2,1)}, bf16[2048,2,128]{2,0,1:T(8,128)(2,1)S(1)}, u32[]{:S(2)}) copy-start(bf16[2048,2,128]{2,0,1:T(8,128)(2,1)S(1)} %get-tuple-element.361) | copy-start | bytes 3145732 | tf_op jit(solution)/shard_map/while
  278.4 2.0 copy-start
  281.5 3.5 copy-start.1
  286.7 2.9 copy-start.2
  289.6 1.7 copy-start.3
  291.3 2.3 copy-start.8
  293.6 6.7 %copy-start.7 = (bf16[2048,2,128]{2,0,1:T(8,128)(2,1)}, bf16[2048,2,128]{2,0,1:T(8,128)(2,1)S(1)}, u32[]{:S(2)}) copy-start(bf16[2048,2,128]{2,0,1:T(8,128)(2,1)S(1)} %get-tuple-element.361) | copy-start | bytes 3145732 | tf_op jit(solution)/shard_map/while
  300.3 2.0 copy-start
  303.4 3.5 copy-start.1
  308.7 2.9 copy-start.2
  313.3 2.3 copy-start.8
  320.8 7.2 %copy-start.4 = (f32[512,2,256]{0,2,1:T(8,128)S(1)}, f32[512,2,256]{0,2,1:T(8,128)}, u32[]{:S(2)}) copy-start(f32[512,2,256]{0,2,1:T(8,128)} %get-tuple-element.73) | copy-start | bytes 3145732
  323.3 26.8 %collective-permute-start.1 = (f32[512,2,256]{2,0,1:T(8,128)}, f32[512,2,256]{2,0,1:T(8,128)}, u32[]{:S(2)}, u32[]{:S(2)}) collective-permute-start(f32[512,2,256]{2,0,1:T(8,128)} %slice_bitcast_fusion), channel_id=1, source_target_pairs={{1,0},{3,2},{5,4},{7,6},{9,8},{11,10},{13,12},{15,14},{17,16},{19,... | collective-permute-start | bytes 3145736 | tf_op jit(solution)/shard_map/ppermute | solution.py:20
  415.4 25.0 %copy-start.9 = (bf16[2,128,4096]{2,1,0:T(8,128)(2,1)S(1)}, bf16[2,128,4096]{2,1,0:T(8,128)(2,1)}, u32[]{:S(2)}) copy-start(bf16[2,128,4096]{2,1,0:T(8,128)(2,1)} %fusion.44) | copy-start | bytes 6291460
  448.5 15.2 %copy-start.15 = (bf16[4,512,2,128]{3,1,0,2:T(8,128)(2,1)S(1)}, bf16[4,512,2,128]{3,1,0,2:T(8,128)(2,1)}, u32[]{:S(2)}) copy-start(bf16[4,512,2,128]{3,1,0,2:T(8,128)(2,1)} %get-tuple-element.71) | copy-start | bytes 3145732
  459.2 27.5 %all-to-all-start.2 = ((bf16[2048,2,128]{2,1,0:T(2,128)(2,1)}), bf16[2048,2,128]{2,1,0:T(2,128)(2,1)S(1)}, u32[]{:S(2)}, u32[]{:S(2)}) async-start(bf16[2048,2,128]{2,1,0:T(2,128)(2,1)} %copy.125), calls=%async_computation.3 | async-start | bytes 2097152 | tf_op jit(solution)/shard_map/all_to_all | solution.py:153
  486.6 56.3 %all-to-all-start.3 = ((bf16[2048,2,128]{2,1,0:T(2,128)(2,1)}), bf16[2048,2,128]{2,1,0:T(2,128)(2,1)S(1)}, u32[]{:S(2)}, u32[]{:S(2)}) async-start(bf16[2048,2,128]{2,1,0:T(2,128)(2,1)} %copy.129), calls=%async_computation.4 | async-start | bytes 2097152 | tf_op jit(solution)/shard_map/all_to_all | solution.py:154
  505.5 41.4 %copy-start.6 = (bf16[2,128,4096]{2,1,0:T(8,128)(2,1)S(1)}, bf16[2,128,4096]{2,1,0:T(8,128)(2,1)}, u32[]{:S(2)}) copy-start(bf16[2,128,4096]{2,1,0:T(8,128)(2,1)} %param.9) | copy-start | bytes 6291460
  505.5 41.4 %copy-start.17 = (f32[4096]{0:T(1024)S(1)}, f32[4096]{0:T(1024)}, u32[]{:S(2)}) copy-start(f32[4096]{0:T(1024)} %copy-done.16) | copy-start | bytes 49156
  505.5 41.4 %copy-start.19 = (s32[4096]{0:T(1024)S(1)}, s32[4096]{0:T(1024)}, u32[]{:S(2)}) copy-start(s32[4096]{0:T(1024)} %copy-done.18) | copy-start | bytes 49156
  505.5 41.4 %copy-start.22 = (f32[2,128]{1,0:T(2,128)S(1)}, f32[2,128]{1,0:T(2,128)}, u32[]{:S(2)}) copy-start(f32[2,128]{1,0:T(2,128)} %copy-done.21) | copy-start | bytes 3076
  546.9 88.4 %copy-start.23 = (f32[2,128]{1,0:T(2,128)S(1)}, f32[2,128]{1,0:T(2,128)}, u32[]{:S(2)}) copy-start(f32[2,128]{1,0:T(2,128)} %get-tuple-element.227) | copy-start | bytes 3076
  (4 other events, 5.1 us)
Sparse Core Ops, SparseCore 0:
  10.1 77.0 all-gather.2
  94.7 18.9 reduce-scatter.2
  116.4 77.6 all-gather.4
  448.6 203.0 reduce-scatter.4
where the time goes:
time: 669 us; the launch traced here: 661 us
  waiting for transfers between devices  229 us (34%)
  blocking collectives  144 us (22%)
  local copies, waits for them, and re-layouts  98.3 us (15%)
  matrix products  68 us (10%)
  other arithmetic  62.6 us (9%)
  starting transfers between devices  41.1 us (6%)
  between operations  14.3 us (2%)
    psum x1, blocking collectives, on_device(): grad_gain = lax.psum(gain_local, 'sp') * seq_length ** (-0.5)  72.5 us
    all_gather x1, waiting for transfers between devices, on_device(): weight_full = lax.all_gather(key_value_weight, 'sp', axis=0, tiled=True)  57.4 us
    all_to_all x1, blocking collectives, on_device(): lax.all_to_all(pair_grad_heads, 'sp', split_axis=0, concat_axis=1, tiled=...  50.7 us
    all_to_all x1, waiting for transfers between devices, on_device(): lax.all_to_all(query_grad_heads, 'sp', split_axis=0, concat_axis=1, tiled...  34.9 us
    all_gather x1, waiting for transfers between devices, on_device(): pair_every = lax.all_gather(pair_heads, 'sp', axis=0, tiled=True)  33.3 us
    all_to_all x1, waiting for transfers between devices, on_device(): lax.all_to_all(grad_tokens, 'sp', split_axis=1, concat_axis=0, tiled=True)  30 us
    ppermute x2, waiting for transfers between devices, shifted(): return lax.ppermute(block, axis, route)  29 us
    reduce_scatter x1, waiting for transfers between devices, on_device(): lax.psum_scatter(jnp.einsum('arf,cf->arc', normed, weight_full, preferred...  19.1 us
  transfers between devices with their start and end apart: 10, of which 9 were waited for; matrix products, arithmetic and copies ran while one was open for 11% of the time, Pallas kernels for 0%

commit v1 on v0

--- a/solution.py
+++ b/solution.py
@@ -12,6 +12,18 @@
 EPS = 1e-05
 KEEP_RATE = 0.9
 MASKED_SCORE = -1e30
+
+
+def resolve_tiles(s0):
+    q_n = lax.psum(1, "sp")
+    parts_seen = [(ix, (ix + 1) % q_n) for ix in range(q_n)]
+    current_value = [None] * q_n
+    current_value[q_n - 1] = s0
+    for u in range(q_n - 2, -1, -1):
+        current_value[u] = lax.ppermute(current_value[u + 1], "sp", perm=parts_seen)
+    side_arr = jnp.concatenate(current_value, axis=0)
+    b_next = (lax.axis_index("sp") + 1) * s0.shape[0]
+    return jnp.roll(side_arr, b_next, axis=0)
 
 
 def shifted(block, axis, distance):
@@ -111,7 +123,7 @@
     inv_rms = lax.rsqrt(square_total[..., None] / D + EPS)
     drop_scale = unpack_flags(keep_bits) / KEEP_RATE
     normed = (input_wide * inv_rms * gain_wide * drop_scale).astype(jnp.bfloat16)
-    weight_full = lax.all_gather(key_value_weight, "sp", axis=0, tiled=True)
+    weight_full = resolve_tiles(key_value_weight)
     pair_tokens = lax.psum_scatter(
         jnp.einsum("arf,cf->arc", normed, weight_full, preferred_element_type=jnp.float32),
         "tp",

time: 669 us -> 774 us (1.16)
  waiting for transfers between devices: 229 us -> 324 us
  local copies, waits for them, and re-layouts: 98.3 us -> 114 us
    ppermute x0 -> x15, waiting for transfers between devices: none -> 153 us  [resolve_tiles(): current_value[u] = lax.ppermute(current_value[u + 1], 'sp', perm=parts_seen)]
    all_gather x1 -> x0, waiting for transfers between devices: 57.4 us -> none  [on_device(): weight_full = lax.all_gather(key_value_weight, 'sp', axis=0, tiled=True)]
    unnamed x41 -> x120, local copies, waits for them, and re-layouts: 11 us -> 26.3 us
  transfers between devices with their start and end apart: 10 -> 24, of which waited for: 9 -> 22; matrix products, arithmetic and copies ran while one was open for 11% -> 10% of each run, Pallas kernels for 0% -> 0%
where the time goes in v1:
time: 774 us; the launch traced here: 766 us
  waiting for transfers between devices  324 us (42%)
  blocking collectives  143 us (18%)
  local copies, waits for them, and re-layouts  114 us (15%)
  matrix products  64.1 us (8%)
  other arithmetic  61.9 us (8%)
  starting transfers between devices  41.7 us (5%)
  between operations  14.8 us (2%)
    ppermute x15, waiting for transfers between devices, resolve_tiles(): current_value[u] = lax.ppermute(current_value[u + 1], 'sp', perm=parts_seen)  153 us
    psum x1, blocking collectives, on_device(): grad_gain = lax.psum(gain_local, 'sp') * seq_length ** (-0.5)  72.4 us
    all_to_all x1, blocking collectives, on_device(): lax.all_to_all(pair_grad_heads, 'sp', split_axis=0, concat_axis=1, tiled=...  50.7 us
    all_to_all x1, waiting for transfers between devices, on_device(): lax.all_to_all(query_grad_heads, 'sp', split_axis=0, concat_axis=1, tiled...  34.9 us
    all_gather x1, waiting for transfers between devices, on_device(): pair_every = lax.all_gather(pair_heads, 'sp', axis=0, tiled=True)  32.9 us
    all_to_all x1, waiting for transfers between devices, on_device(): lax.all_to_all(grad_tokens, 'sp', split_axis=1, concat_axis=0, tiled=True)  30 us
    ppermute x2, waiting for transfers between devices, shifted(): return lax.ppermute(block, axis, route)  29.5 us
    unnamed x120, local copies, waits for them, and re-layouts  26.3 us
  transfers between devices with their start and end apart: 24, of which 22 were waited for; matrix products, arithmetic and copies ran while one was open for 10% of the time, Pallas kernels for 0%

profile of v1, /device:TPU:0, one launch (start us, length us, event | category | flops | bytes accessed | tf_op | source)
XLA Modules:
  0.0 765.7 jit_solution(9001245147967531772)
XLA Ops:
  7.8 12.0 %collective-permute-done = bf16[64,4096]{1,0:T(8,128)(2,1)S(1)} collective-permute-done((bf16[64,4096]{1,0:T(8,128)(2,1)}, bf16[64,4096]{1,0:T(8,128)(2,1)S(1)}, u32[]{:S(2)}, u32[]{:S(2)}) %collective-permute-start) | collective-permute-done | bytes 524320 | tf_op jit(solution)/shard_map/ppermute | solution.py:23
  19.8 11.3 %collective-permute-done.1 = bf16[64,4096]{1,0:T(8,128)(2,1)S(1)} collective-permute-done((bf16[64,4096]{1,0:T(8,128)(2,1)S(1)}, bf16[64,4096]{1,0:T(8,128)(2,1)S(1)}, u32[]{:S(2)}, u32[]{:S(2)}) %collective-permute-start.1) | collective-permute-done | bytes 524320 | tf_op jit(solution)/shard_map/ppermute | solution.py:23
  31.1 11.3 %collective-permute-done.2 = bf16[64,4096]{1,0:T(8,128)(2,1)S(1)} collective-permute-done((bf16[64,4096]{1,0:T(8,128)(2,1)S(1)}, bf16[64,4096]{1,0:T(8,128)(2,1)S(1)}, u32[]{:S(2)}, u32[]{:S(2)}) %collective-permute-start.2) | collective-permute-done | bytes 524320 | tf_op jit(solution)/shard_map/ppermute | solution.py:23
  42.4 11.3 %collective-permute-done.3 = bf16[64,4096]{1,0:T(8,128)(2,1)S(1)} collective-permute-done((bf16[64,4096]{1,0:T(8,128)(2,1)S(1)}, bf16[64,4096]{1,0:T(8,128)(2,1)S(1)}, u32[]{:S(2)}, u32[]{:S(2)}) %collective-permute-start.3) | collective-permute-done | bytes 524320 | tf_op jit(solution)/shard_map/ppermute | solution.py:23
  53.7 11.3 %collective-permute-done.4 = bf16[64,4096]{1,0:T(8,128)(2,1)S(1)} collective-permute-done((bf16[64,4096]{1,0:T(8,128)(2,1)S(1)}, bf16[64,4096]{1,0:T(8,128)(2,1)S(1)}, u32[]{:S(2)}, u32[]{:S(2)}) %collective-permute-start.4) | collective-permute-done | bytes 524320 | tf_op jit(solution)/shard_map/ppermute | solution.py:23
  65.0 11.3 %collective-permute-done.5 = bf16[64,4096]{1,0:T(8,128)(2,1)S(1)} collective-permute-done((bf16[64,4096]{1,0:T(8,128)(2,1)S(1)}, bf16[64,4096]{1,0:T(8,128)(2,1)S(1)}, u32[]{:S(2)}, u32[]{:S(2)}) %collective-permute-start.5) | collective-permute-done | bytes 524320 | tf_op jit(solution)/shard_map/ppermute | solution.py:23
  76.3 11.3 %collective-permute-done.6 = bf16[64,4096]{1,0:T(8,128)(2,1)S(1)} collective-permute-done((bf16[64,4096]{1,0:T(8,128)(2,1)S(1)}, bf16[64,4096]{1,0:T(8,128)(2,1)S(1)}, u32[]{:S(2)}, u32[]{:S(2)}) %collective-permute-start.6) | collective-permute-done | bytes 524320 | tf_op jit(solution)/shard_map/ppermute | solution.py:23
  87.6 11.3 %collective-permute-done.7 = bf16[64,4096]{1,0:T(8,128)(2,1)S(1)} collective-permute-done((bf16[64,4096]{1,0:T(8,128)(2,1)S(1)}, bf16[64,4096]{1,0:T(8,128)(2,1)S(1)}, u32[]{:S(2)}, u32[]{:S(2)}) %collective-permute-start.7) | collective-permute-done | bytes 524320 | tf_op jit(solution)/shard_map/ppermute | solution.py:23
  98.9 11.3 %collective-permute-done.8 = bf16[64,4096]{1,0:T(8,128)(2,1)S(1)} collective-permute-done((bf16[64,4096]{1,0:T(8,128)(2,1)S(1)}, bf16[64,4096]{1,0:T(8,128)(2,1)S(1)}, u32[]{:S(2)}, u32[]{:S(2)}) %collective-permute-start.8) | collective-permute-done | bytes 524320 | tf_op jit(solution)/shard_map/ppermute | solution.py:23
  110.2 11.3 %collective-permute-done.9 = bf16[64,4096]{1,0:T(8,128)(2,1)S(1)} collective-permute-done((bf16[64,4096]{1,0:T(8,128)(2,1)S(1)}, bf16[64,4096]{1,0:T(8,128)(2,1)S(1)}, u32[]{:S(2)}, u32[]{:S(2)}) %collective-permute-start.9) | collective-permute-done | bytes 524320 | tf_op jit(solution)/shard_map/ppermute | solution.py:23
  121.5 11.3 %collective-permute-done.10 = bf16[64,4096]{1,0:T(8,128)(2,1)S(1)} collective-permute-done((bf16[64,4096]{1,0:T(8,128)(2,1)S(1)}, bf16[64,4096]{1,0:T(8,128)(2,1)S(1)}, u32[]{:S(2)}, u32[]{:S(2)}) %collective-permute-start.10) | collective-permute-done | bytes 524320 | tf_op jit(solution)/shard_map/ppermute | solution.py:23
  132.9 11.3 %collective-permute-done.11 = bf16[64,4096]{1,0:T(8,128)(2,1)S(1)} collective-permute-done((bf16[64,4096]{1,0:T(8,128)(2,1)S(1)}, bf16[64,4096]{1,0:T(8,128)(2,1)S(1)}, u32[]{:S(2)}, u32[]{:S(2)}) %collective-permute-start.11) | collective-permute-done | bytes 524320 | tf_op jit(solution)/shard_map/ppermute | solution.py:23
  145.7 10.0 %collective-permute-done.12 = bf16[64,4096]{1,0:T(8,128)(2,1)} collective-permute-done((bf16[64,4096]{1,0:T(8,128)(2,1)S(1)}, bf16[64,4096]{1,0:T(8,128)(2,1)}, u32[]{:S(2)}, u32[]{:S(2)}) %collective-permute-start.12) | collective-permute-done | bytes 524320 | tf_op jit(solution)/shard_map/ppermute | solution.py:23
  158.0 5.8 copy.119
  164.5 4.9 psum.21
  170.0 4.7 fusion.46
  174.7 6.8 collective-permute-done.14
  191.2 5.8 copy-done.43
  197.1 3.3 fusion.36
  200.5 18.2 %reduce-scatter.3.cloned.1.call-done = f32[1,128,1024]{2,1,0:T(8,128)} async-done(((f32[2,128,1024]{2,1,0:T(8,128)}), f32[1,128,1024]{2,1,0:T(8,128)}) %reduce-scatter.3.cloned.1.call-update) | async-done | bytes 524304 | tf_op jit(solution)/shard_map/reduce_scatter | solution.py:127
  222.0 5.6 all-to-all-start.1
  229.0 30.0 %all-to-all-done.1 = bf16[128,32,128]{0,2,1:T(8,128)(2,1)S(1)} async-done(((bf16[128,32,128]{0,2,1:T(8,128)(2,1)}), bf16[128,32,128]{0,2,1:T(8,128)(2,1)S(1)}, u32[]{:S(2)}, u32[]{:S(2)}) %all-to-all-start.1) | async-done | bytes 1048608 | tf_op jit(solution)/shard_map/all_to_all | solution.py:146
  258.9 6.8 all-to-all-start
  266.3 32.9 %all-gather.2.cloned.1.call-done = bf16[2048,4,256]{2,1,0:T(4,128)(2,1)} async-done(((bf16[128,4,256]{2,1,0:T(4,128)(2,1)}), bf16[2048,4,256]{2,1,0:T(4,128)(2,1)}) %all-gather.2.cloned.1.call-update) | async-done | bytes 4194320 | tf_op jit(solution)/shard_map/all_gather | solution.py:137
  299.2 4.6 fusion.54
  306.3 4.6 collective-permute-start.15
  313.0 8.9 %collective-permute-done.15 = bf16[512,2,256]{2,1,0:T(2,128)(2,1)} collective-permute-done((bf16[512,2,256]{2,1,0:T(2,128)(2,1)}, bf16[512,2,256]{2,1,0:T(2,128)(2,1)}, u32[]{:S(2)}, u32[]{:S(2)}) %collective-permute-start.15) | collective-permute-done | bytes 524320 | tf_op jit(solution)/shard_map/ppermute | solution.py:32
  322.0 9.7 %pad_maximum_fusion.1 = bf16[2560,2,256]{2,1,0:T(2,128)(2,1)} fusion(bf16[2048,2,256]{2,1,0:T(2,128)(2,1)} %copy-done.11, bf16[512,2,256]{2,1,0:T(2,128)(2,1)} %collective-permute-done.15), kind=kLoop, calls=%fused_computation.79 | loop fusion | flops 1310720 | bytes 5242880 | tf_op jit(solution)/shard_map/concatenate | solution.py:148
  332.8 87.8 %while.17 = (s32[]{:T(128)}, f32[512,2,256]{0,2,1:T(8,128)}, bf16[4,512,2,128]{3,1,0,2:T(8,128)(2,1)}, bf16[4,512,2,128]{3,1,0,2:T(8,128)(2,1)}, f32[4,512,2,256...) while((s32[]{:T(128)}, f32[512,2,256]{0,2,1:T(8,128)}, ...), condition=%wide.region_7.8_spmd.clone, body=%wide.region_3.7_spmd.clone.sunk | while | flops 1631453184 | bytes 125355472 | solution.py:105
  420.6 5.3 copy.133
  429.7 3.3 copy.132
  434.4 20.6 %collective-permute-done.16 = f32[512,2,256]{2,0,1:T(8,128)} collective-permute-done((f32[512,2,256]{2,0,1:T(8,128)}, f32[512,2,256]{2,0,1:T(8,128)}, u32[]{:S(2)}, u32[]{:S(2)}) %collective-permute-start.16) | collective-permute-done | bytes 1048608 | tf_op jit(solution)/shard_map/ppermute | solution.py:32
  456.8 12.8 %copy.135 = bf16[2048,2,256]{2,1,0:T(2,128)(2,1)S(1)} copy(bf16[2048,2,256]{2,0,1:T(8,128)(2,1)S(1)} %pad_maximum_fusion.2) | data formatting | bytes 4194304 | tf_op jit(solution)/shard_map/concatenate | solution.py:159
  469.6 50.7 %all_to_all.75 = bf16[2048,2,256]{2,1,0:T(2,128)(2,1)S(1)} all-to-all(bf16[2048,2,256]{2,1,0:T(2,128)(2,1)S(1)} %copy.135), channel_id=1, replica_groups=mesh['sp'=16,'tp'=2] {'sp'}, dimensions={0} | all-to-all | bytes 4194304 | tf_op jit(solution)/shard_map/all_to_all | solution.py:167
  520.3 12.2 %convert_reduce_fusion = f32[2048,256]{1,0:T(8,128)} fusion(bf16[2048,2,256]{2,1,0:T(2,128)(2,1)S(1)} %all_to_all.75), kind=kLoop, calls=%fused_computation.74 | loop fusion | flops 1572864 | bytes 4194304 | tf_op jit(solution)/shard_map/reduce_sum | solution.py:43
  534.7 9.8 %all_gather.7 = bf16[2,128,1024]{2,1,0:T(8,128)(2,1)S(1)} all-gather(bf16[1,128,1024]{2,1,0:T(8,128)(2,1)S(1)} %copy.137), channel_id=1, replica_groups=mesh['sp'=16,'tp'=2] {'tp'}, dimensions={0}, use_global_device_ids=true | all-gather | bytes 786432 | tf_op jit(solution)/shard_map/all_gather | solution.py:170
  545.3 8.2 %convolution_bitcast_fusion.1 = f32[1024,4096]{1,0:T(8,128)} fusion(bf16[2,128,1024]{2,1,0:T(8,128)(2,1)S(1)} %all_gather.7, bf16[2,128,4096]{2,1,0:T(8,128)(2,1)S(1)} %copy-done.10), kind=kOutput, calls=%fused_computation.50 | convolution fusion | flops 2147483648 | bytes 19398656 | tf_op jit(solution)/shard_map/arc,arf->cf/dot_general | solution.py:175
  554.7 9.4 %copy.125 = bf16[2048,2,128]{2,1,0:T(2,128)(2,1)} copy(bf16[2048,2,128]{2,0,1:T(8,128)(2,1)S(1)} %bitcast.97) | data formatting | bytes 2097152 | tf_op jit(solution)/shard_map/reshape | solution.py:162
  564.1 4.6 all-to-all-start.2
  568.7 9.5 %copy.129 = bf16[2048,2,128]{2,1,0:T(2,128)(2,1)} copy(bf16[2048,2,128]{2,0,1:T(8,128)(2,1)S(1)} %bitcast.98) | data formatting | bytes 2097152 | tf_op jit(solution)/shard_map/reshape | solution.py:163
  578.2 13.4 %all-to-all-done.2 = bf16[2048,2,128]{2,1,0:T(2,128)(2,1)S(1)} async-done(((bf16[2048,2,128]{2,1,0:T(2,128)(2,1)}), bf16[2048,2,128]{2,1,0:T(2,128)(2,1)S(1)}, u32[]{:S(2)}, u32[]{:S(2)}) %all-to-all-start.2) | async-done | bytes 1048608 | tf_op jit(solution)/shard_map/all_to_all | solution.py:165
  591.6 17.4 %all-to-all-start.3 = ((bf16[2048,2,128]{2,1,0:T(2,128)(2,1)}), bf16[2048,2,128]{2,1,0:T(2,128)(2,1)S(1)}, u32[]{:S(2)}, u32[]{:S(2)}) async-start(bf16[2048,2,128]{2,1,0:T(2,128)(2,1)} %copy.129), calls=%async_computation.4 | async-start | bytes 2097152 | tf_op jit(solution)/shard_map/all_to_all | solution.py:166
  612.9 34.9 %all-to-all-done.3 = bf16[2048,2,128]{2,1,0:T(2,128)(2,1)S(1)} async-done(((bf16[2048,2,128]{2,1,0:T(2,128)(2,1)}), bf16[2048,2,128]{2,1,0:T(2,128)(2,1)S(1)}, u32[]{:S(2)}, u32[]{:S(2)}) %all-to-all-start.3) | async-done | bytes 1048608 | tf_op jit(solution)/shard_map/all_to_all | solution.py:166
  651.9 10.4 %fusion.53 = (f32[4096]{0:T(1024)S(1)}, f32[2,128]{1,0:T(2,128)S(1)}, f32[2,128,4096]{2,1,0:T(8,128)}) fusion(bf16[2,128,4096]{2,1,0:T(8,128)(2,1)S(1)} %copy-done.6, f32[2,128]{1,0:T(2,128)S(1)} %copy-done.45, f32[4096]{0:T(1024)S(1)} %copy-done.39, s32[2,128,4096]{2,1,0:T(8,128)} %copy.119, s32[4096]{0:T(1024)S(1)} %copy-done.41, ...), kind=kOutput, calls=%fused_computation.73 | convolution fusion | flops 2160062208 | bytes 19449860 | tf_op jit(solution)/shard_map/arc,cf->arf/dot_general | solution.py:171
  662.3 4.9 psum.22
  667.2 72.4 %psum.23 = f32[4096]{0:T(1024)S(1)} all-reduce(f32[4096]{0:T(1024)S(1)} %get-tuple-element.193), channel_id=1, replica_groups=mesh['sp'=16,'tp'=2] {'sp'}, use_global_device_ids=true, to_apply=%region_14.15 | all-reduce | flops 4096 | bytes 32768 | tf_op jit(solution)/shard_map/psum | solution.py:187
  740.3 4.9 fusion.50
  745.2 11.5 %reduce-scatter.5.cloned.1.call-done = f32[64,4096]{1,0:T(8,128)} async-done(((f32[1024,4096]{1,0:T(8,128)}), f32[64,4096]{1,0:T(8,128)}) %reduce-scatter.5.cloned.1.call-update) | async-done | bytes 1048592 | tf_op jit(solution)/shard_map/reduce_scatter | solution.py:174
  (298 shorter events, 132.4 us)
Async XLA Ops:
  7.2 150.8 %copy-start.46 = (bf16[4096]{0:T(1024)(128)(2,1)S(1)}, bf16[4096]{0:T(1024)(128)(2,1)}, u32[]{:S(2)}) copy-start(bf16[4096]{0:T(1024)(128)(2,1)} %param.10) | copy-start | bytes 24580
  7.2 211.6 %reduce-scatter.3.cloned.1.call-start = ((), (), s32[]{:S(2)}) async-start(), calls=%async_computation.7 | async-start | bytes 1572864 | tf_op jit(solution)/shard_map/reduce_scatter | solution.py:127
  7.2 12.6 %collective-permute-start = (bf16[64,4096]{1,0:T(8,128)(2,1)}, bf16[64,4096]{1,0:T(8,128)(2,1)S(1)}, u32[]{:S(2)}, u32[]{:S(2)}) collective-permute-start(bf16[64,4096]{1,0:T(8,128)(2,1)} %param.12), channel_id=1, source_target_pairs={{0,2},{2,4},{4,6},{6,8},{8,10},{10,12},{12,14},{14,16},{16,18},{18... | collective-permute-start | bytes 1572872 | tf_op jit(solution)/shard_map/ppermute | solution.py:23
  19.8 11.3 %collective-permute-start.1 = (bf16[64,4096]{1,0:T(8,128)(2,1)S(1)}, bf16[64,4096]{1,0:T(8,128)(2,1)S(1)}, u32[]{:S(2)}, u32[]{:S(2)}) collective-permute-start(bf16[64,4096]{1,0:T(8,128)(2,1)S(1)} %collective-permute-done), channel_id=1, source_target_pairs={{0,2},{2,4},{4,6},{6,8},{8,10},{10,12},{12,14},{14,16},{16,18},{18... | collective-permute-start | bytes 1572872 | tf_op jit(solution)/shard_map/ppermute | solution.py:23
  31.1 11.3 %collective-permute-start.2 = (bf16[64,4096]{1,0:T(8,128)(2,1)S(1)}, bf16[64,4096]{1,0:T(8,128)(2,1)S(1)}, u32[]{:S(2)}, u32[]{:S(2)}) collective-permute-start(bf16[64,4096]{1,0:T(8,128)(2,1)S(1)} %collective-permute-done.1), channel_id=1, source_target_pairs={{0,2},{2,4},{4,6},{6,8},{8,10},{10,12},{12,14},{14,16},{16,18},{18... | collective-permute-start | bytes 1572872 | tf_op jit(solution)/shard_map/ppermute | solution.py:23
  42.4 101.8 %copy-start.14 = (bf16[64,4096]{1,0:T(8,128)(2,1)}, bf16[64,4096]{1,0:T(8,128)(2,1)S(1)}, u32[]{:S(2)}) copy-start(bf16[64,4096]{1,0:T(8,128)(2,1)S(1)} %collective-permute-done.2) | copy-start | bytes 1572868
  42.4 11.3 %collective-permute-start.3 = (bf16[64,4096]{1,0:T(8,128)(2,1)S(1)}, bf16[64,4096]{1,0:T(8,128)(2,1)S(1)}, u32[]{:S(2)}, u32[]{:S(2)}) collective-permute-start(bf16[64,4096]{1,0:T(8,128)(2,1)S(1)} %collective-permute-done.2), channel_id=1, source_target_pairs={{0,2},{2,4},{4,6},{6,8},{8,10},{10,12},{12,14},{14,16},{16,18},{18... | collective-permute-start | bytes 1572872 | tf_op jit(solution)/shard_map/ppermute | solution.py:23
  53.7 90.5 %copy-start.16 = (bf16[64,4096]{1,0:T(8,128)(2,1)}, bf16[64,4096]{1,0:T(8,128)(2,1)S(1)}, u32[]{:S(2)}) copy-start(bf16[64,4096]{1,0:T(8,128)(2,1)S(1)} %collective-permute-done.3) | copy-start | bytes 1572868
  53.7 11.3 %collective-permute-start.4 = (bf16[64,4096]{1,0:T(8,128)(2,1)S(1)}, bf16[64,4096]{1,0:T(8,128)(2,1)S(1)}, u32[]{:S(2)}, u32[]{:S(2)}) collective-permute-start(bf16[64,4096]{1,0:T(8,128)(2,1)S(1)} %collective-permute-done.3), channel_id=1, source_target_pairs={{0,2},{2,4},{4,6},{6,8},{8,10},{10,12},{12,14},{14,16},{16,18},{18... | collective-permute-start | bytes 1572872 | tf_op jit(solution)/shard_map/ppermute | solution.py:23
  65.0 79.1 %copy-start.18 = (bf16[64,4096]{1,0:T(8,128)(2,1)}, bf16[64,4096]{1,0:T(8,128)(2,1)S(1)}, u32[]{:S(2)}) copy-start(bf16[64,4096]{1,0:T(8,128)(2,1)S(1)} %collective-permute-done.4) | copy-start | bytes 1572868
  65.0 11.3 %collective-permute-start.5 = (bf16[64,4096]{1,0:T(8,128)(2,1)S(1)}, bf16[64,4096]{1,0:T(8,128)(2,1)S(1)}, u32[]{:S(2)}, u32[]{:S(2)}) collective-permute-start(bf16[64,4096]{1,0:T(8,128)(2,1)S(1)} %collective-permute-done.4), channel_id=1, source_target_pairs={{0,2},{2,4},{4,6},{6,8},{8,10},{10,12},{12,14},{14,16},{16,18},{18... | collective-permute-start | bytes 1572872 | tf_op jit(solution)/shard_map/ppermute | solution.py:23
  76.3 67.8 %copy-start.20 = (bf16[64,4096]{1,0:T(8,128)(2,1)}, bf16[64,4096]{1,0:T(8,128)(2,1)S(1)}, u32[]{:S(2)}) copy-start(bf16[64,4096]{1,0:T(8,128)(2,1)S(1)} %collective-permute-done.5) | copy-start | bytes 1572868
  76.3 11.3 %collective-permute-start.6 = (bf16[64,4096]{1,0:T(8,128)(2,1)S(1)}, bf16[64,4096]{1,0:T(8,128)(2,1)S(1)}, u32[]{:S(2)}, u32[]{:S(2)}) collective-permute-start(bf16[64,4096]{1,0:T(8,128)(2,1)S(1)} %collective-permute-done.5), channel_id=1, source_target_pairs={{0,2},{2,4},{4,6},{6,8},{8,10},{10,12},{12,14},{14,16},{16,18},{18... | collective-permute-start | bytes 1572872 | tf_op jit(solution)/shard_map/ppermute | solution.py:23
  87.6 56.6 %copy-start.22 = (bf16[64,4096]{1,0:T(8,128)(2,1)}, bf16[64,4096]{1,0:T(8,128)(2,1)S(1)}, u32[]{:S(2)}) copy-start(bf16[64,4096]{1,0:T(8,128)(2,1)S(1)} %collective-permute-done.6) | copy-start | bytes 1572868
  87.6 11.3 %collective-permute-start.7 = (bf16[64,4096]{1,0:T(8,128)(2,1)S(1)}, bf16[64,4096]{1,0:T(8,128)(2,1)S(1)}, u32[]{:S(2)}, u32[]{:S(2)}) collective-permute-start(bf16[64,4096]{1,0:T(8,128)(2,1)S(1)} %collective-permute-done.6), channel_id=1, source_target_pairs={{0,2},{2,4},{4,6},{6,8},{8,10},{10,12},{12,14},{14,16},{16,18},{18... | collective-permute-start | bytes 1572872 | tf_op jit(solution)/shard_map/ppermute | solution.py:23
  98.9 45.3 %copy-start.24 = (bf16[64,4096]{1,0:T(8,128)(2,1)}, bf16[64,4096]{1,0:T(8,128)(2,1)S(1)}, u32[]{:S(2)}) copy-start(bf16[64,4096]{1,0:T(8,128)(2,1)S(1)} %collective-permute-done.7) | copy-start | bytes 1572868
  98.9 11.3 %collective-permute-start.8 = (bf16[64,4096]{1,0:T(8,128)(2,1)S(1)}, bf16[64,4096]{1,0:T(8,128)(2,1)S(1)}, u32[]{:S(2)}, u32[]{:S(2)}) collective-permute-start(bf16[64,4096]{1,0:T(8,128)(2,1)S(1)} %collective-permute-done.7), channel_id=1, source_target_pairs={{0,2},{2,4},{4,6},{6,8},{8,10},{10,12},{12,14},{14,16},{16,18},{18... | collective-permute-start | bytes 1572872 | tf_op jit(solution)/shard_map/ppermute | solution.py:23
  110.2 34.0 %copy-start.26 = (bf16[64,4096]{1,0:T(8,128)(2,1)}, bf16[64,4096]{1,0:T(8,128)(2,1)S(1)}, u32[]{:S(2)}) copy-start(bf16[64,4096]{1,0:T(8,128)(2,1)S(1)} %collective-permute-done.8) | copy-start | bytes 1572868
  110.2 11.3 %collective-permute-start.9 = (bf16[64,4096]{1,0:T(8,128)(2,1)S(1)}, bf16[64,4096]{1,0:T(8,128)(2,1)S(1)}, u32[]{:S(2)}, u32[]{:S(2)}) collective-permute-start(bf16[64,4096]{1,0:T(8,128)(2,1)S(1)} %collective-permute-done.8), channel_id=1, source_target_pairs={{0,2},{2,4},{4,6},{6,8},{8,10},{10,12},{12,14},{14,16},{16,18},{18... | collective-permute-start | bytes 1572872 | tf_op jit(solution)/shard_map/ppermute | solution.py:23
  121.5 22.7 %copy-start.28 = (bf16[64,4096]{1,0:T(8,128)(2,1)}, bf16[64,4096]{1,0:T(8,128)(2,1)S(1)}, u32[]{:S(2)}) copy-start(bf16[64,4096]{1,0:T(8,128)(2,1)S(1)} %collective-permute-done.9) | copy-start | bytes 1572868
  121.5 11.3 %collective-permute-start.10 = (bf16[64,4096]{1,0:T(8,128)(2,1)S(1)}, bf16[64,4096]{1,0:T(8,128)(2,1)S(1)}, u32[]{:S(2)}, u32[]{:S(2)}) collective-permute-start(bf16[64,4096]{1,0:T(8,128)(2,1)S(1)} %collective-permute-done.9), channel_id=1, source_target_pairs={{0,2},{2,4},{4,6},{6,8},{8,10},{10,12},{12,14},{14,16},{16,18},{18... | collective-permute-start | bytes 1572872 | tf_op jit(solution)/shard_map/ppermute | solution.py:23
  132.9 11.3 %collective-permute-start.11 = (bf16[64,4096]{1,0:T(8,128)(2,1)S(1)}, bf16[64,4096]{1,0:T(8,128)(2,1)S(1)}, u32[]{:S(2)}, u32[]{:S(2)}) collective-permute-start(bf16[64,4096]{1,0:T(8,128)(2,1)S(1)} %collective-permute-done.10), channel_id=1, source_target_pairs={{0,2},{2,4},{4,6},{6,8},{8,10},{10,12},{12,14},{14,16},{16,18},{18... | collective-permute-start | bytes 1572872 | tf_op jit(solution)/shard_map/ppermute | solution.py:23
  144.2 13.7 %copy-start.32 = (bf16[64,4096]{1,0:T(8,128)(2,1)}, bf16[64,4096]{1,0:T(8,128)(2,1)S(1)}, u32[]{:S(2)}) copy-start(bf16[64,4096]{1,0:T(8,128)(2,1)S(1)} %collective-permute-done.11) | copy-start | bytes 1572868
  144.2 11.5 %collective-permute-start.12 = (bf16[64,4096]{1,0:T(8,128)(2,1)S(1)}, bf16[64,4096]{1,0:T(8,128)(2,1)}, u32[]{:S(2)}, u32[]{:S(2)}) collective-permute-start(bf16[64,4096]{1,0:T(8,128)(2,1)S(1)} %collective-permute-done.11), channel_id=1, source_target_pairs={{0,2},{2,4},{4,6},{6,8},{8,10},{10,12},{12,14},{14,16},{16,18},{18... | collective-permute-start | bytes 1572872 | tf_op jit(solution)/shard_map/ppermute | solution.py:23
  155.7 14.2 %collective-permute-start.13 = (bf16[64,4096]{1,0:T(8,128)(2,1)}, bf16[64,4096]{1,0:T(8,128)(2,1)}, u32[]{:S(2)}, u32[]{:S(2)}) collective-permute-start(bf16[64,4096]{1,0:T(8,128)(2,1)} %collective-permute-done.12), channel_id=1, source_target_pairs={{0,2},{2,4},{4,6},{6,8},{8,10},{10,12},{12,14},{14,16},{16,18},{18... | collective-permute-start | bytes 1572872 | tf_op jit(solution)/shard_map/ppermute | solution.py:23
  157.9 12.0 %copy-start.38 = (f32[4096]{0:T(1024)}, f32[4096]{0:T(1024)S(1)}, u32[]{:S(2)}) copy-start(f32[4096]{0:T(1024)S(1)} %convert_element_type.69) | copy-start | bytes 49156
  169.9 11.6 %collective-permute-start.14 = (bf16[64,4096]{1,0:T(8,128)(2,1)}, bf16[64,4096]{1,0:T(8,128)(2,1)}, u32[]{:S(2)}, u32[]{:S(2)}) collective-permute-start(bf16[64,4096]{1,0:T(8,128)(2,1)} %collective-permute-done.13), channel_id=1, source_target_pairs={{0,2},{2,4},{4,6},{6,8},{8,10},{10,12},{12,14},{14,16},{16,18},{18... | collective-permute-start | bytes 1572872 | tf_op jit(solution)/shard_map/ppermute | solution.py:23
  174.7 11.5 %copy-start.27 = (bf16[64,4096]{1,0:T(8,128)(2,1)S(1)}, bf16[64,4096]{1,0:T(8,128)(2,1)}, u32[]{:S(2)}) copy-start(bf16[64,4096]{1,0:T(8,128)(2,1)} %copy-done.26) | copy-start | bytes 1572868
  174.7 11.6 %copy-start.25 = (bf16[64,4096]{1,0:T(8,128)(2,1)S(1)}, bf16[64,4096]{1,0:T(8,128)(2,1)}, u32[]{:S(2)}) copy-start(bf16[64,4096]{1,0:T(8,128)(2,1)} %copy-done.24) | copy-start | bytes 1572868
  174.7 11.6 %copy-start.23 = (bf16[64,4096]{1,0:T(8,128)(2,1)S(1)}, bf16[64,4096]{1,0:T(8,128)(2,1)}, u32[]{:S(2)}) copy-start(bf16[64,4096]{1,0:T(8,128)(2,1)} %copy-done.22) | copy-start | bytes 1572868
  197.1 23.6 %copy-start.34 = (bf16[1,128,4096]{2,1,0:T(8,128)(2,1)S(1)}, bf16[1,128,4096]{2,1,0:T(8,128)(2,1)}, u32[]{:S(2)}) copy-start(bf16[1,128,4096]{2,1,0:T(8,128)(2,1)} %param.15) | copy-start | bytes 3145732
  200.4 27.2 %copy-start.35 = (bf16[1,128,4096]{2,1,0:T(8,128)(2,1)S(1)}, bf16[1,128,4096]{2,1,0:T(8,128)(2,1)}, u32[]{:S(2)}) copy-start(bf16[1,128,4096]{2,1,0:T(8,128)(2,1)} %param.13) | copy-start | bytes 3145732
  200.4 98.7 %all-gather.2.cloned.1.call-start = ((), (), s32[]{:S(2)}) async-start(), calls=%async_computation.8 | async-start | bytes 4456448 | tf_op jit(solution)/shard_map/all_gather | solution.py:137
  222.0 36.9 %all-to-all-start.1 = ((bf16[128,32,128]{0,2,1:T(8,128)(2,1)}), bf16[128,32,128]{0,2,1:T(8,128)(2,1)S(1)}, u32[]{:S(2)}, u32[]{:S(2)}) async-start(bf16[128,32,128]{0,2,1:T(8,128)(2,1)} %bitcast.9), calls=%async_computation.2 | async-start | bytes 2097152 | tf_op jit(solution)/shard_map/all_to_all | solution.py:146
  258.9 53.4 %all-to-all-start = ((bf16[128,32,128]{0,2,1:T(8,128)(2,1)}), bf16[128,32,128]{0,2,1:T(8,128)(2,1)S(1)}, u32[]{:S(2)}, u32[]{:S(2)}) async-start(bf16[128,32,128]{0,2,1:T(8,128)(2,1)} %bitcast), calls=%async_computation | async-start | bytes 2097152 | tf_op jit(solution)/shard_map/all_to_all | solution.py:136
  265.7 490.9 %reduce-scatter.5.cloned.1.call-start = ((), (), s32[]{:S(2)}) async-start(), calls=%async_computation.9 | async-start | bytes 17825792 | tf_op jit(solution)/shard_map/reduce_scatter | solution.py:174
  266.3 44.6 %copy-start.42 = (s32[4096]{0:T(1024)S(1)}, s32[4096]{0:T(1024)}, u32[]{:S(2)}) copy-start(s32[4096]{0:T(1024)} %param.14) | copy-start | bytes 49156
  306.3 15.7 %collective-permute-start.15 = (bf16[512,2,256]{2,1,0:T(2,128)(2,1)}, bf16[512,2,256]{2,1,0:T(2,128)(2,1)}, u32[]{:S(2)}, u32[]{:S(2)}) collective-permute-start(bf16[512,2,256]{2,1,0:T(2,128)(2,1)} %slice.35), channel_id=1, source_target_pairs={{0,1},{2,3},{4,5},{6,7},{8,9},{10,11},{12,13},{14,15},{16,17},{18,... | collective-permute-start | bytes 1572872 | tf_op jit(solution)/shard_map/ppermute | solution.py:32
  428.2 26.8 %collective-permute-start.16 = (f32[512,2,256]{2,0,1:T(8,128)}, f32[512,2,256]{2,0,1:T(8,128)}, u32[]{:S(2)}, u32[]{:S(2)}) collective-permute-start(f32[512,2,256]{2,0,1:T(8,128)} %slice_bitcast_fusion), channel_id=1, source_target_pairs={{1,0},{3,2},{5,4},{7,6},{9,8},{11,10},{13,12},{15,14},{17,16},{19,... | collective-permute-start | bytes 3145736 | tf_op jit(solution)/shard_map/ppermute | solution.py:32
  520.3 25.0 %copy-start.10 = (bf16[2,128,4096]{2,1,0:T(8,128)(2,1)S(1)}, bf16[2,128,4096]{2,1,0:T(8,128)(2,1)}, u32[]{:S(2)}) copy-start(bf16[2,128,4096]{2,1,0:T(8,128)(2,1)} %fusion.46) | copy-start | bytes 6291460
  553.5 15.2 %copy-start.37 = (bf16[4,512,2,128]{3,1,0,2:T(8,128)(2,1)S(1)}, bf16[4,512,2,128]{3,1,0,2:T(8,128)(2,1)}, u32[]{:S(2)}) copy-start(bf16[4,512,2,128]{3,1,0,2:T(8,128)(2,1)} %get-tuple-element.71) | copy-start | bytes 3145732
  564.1 27.5 %all-to-all-start.2 = ((bf16[2048,2,128]{2,1,0:T(2,128)(2,1)}), bf16[2048,2,128]{2,1,0:T(2,128)(2,1)S(1)}, u32[]{:S(2)}, u32[]{:S(2)}) async-start(bf16[2048,2,128]{2,1,0:T(2,128)(2,1)} %copy.125), calls=%async_computation.3 | async-start | bytes 2097152 | tf_op jit(solution)/shard_map/all_to_all | solution.py:165
  591.6 56.3 %all-to-all-start.3 = ((bf16[2048,2,128]{2,1,0:T(2,128)(2,1)}), bf16[2048,2,128]{2,1,0:T(2,128)(2,1)S(1)}, u32[]{:S(2)}, u32[]{:S(2)}) async-start(bf16[2048,2,128]{2,1,0:T(2,128)(2,1)} %copy.129), calls=%async_computation.4 | async-start | bytes 2097152 | tf_op jit(solution)/shard_map/all_to_all | solution.py:166
  610.5 41.4 %copy-start.6 = (bf16[2,128,4096]{2,1,0:T(8,128)(2,1)S(1)}, bf16[2,128,4096]{2,1,0:T(8,128)(2,1)}, u32[]{:S(2)}) copy-start(bf16[2,128,4096]{2,1,0:T(8,128)(2,1)} %param.9) | copy-start | bytes 6291460
  610.5 41.4 %copy-start.39 = (f32[4096]{0:T(1024)S(1)}, f32[4096]{0:T(1024)}, u32[]{:S(2)}) copy-start(f32[4096]{0:T(1024)} %copy-done.38) | copy-start | bytes 49156
  610.5 41.4 %copy-start.41 = (s32[4096]{0:T(1024)S(1)}, s32[4096]{0:T(1024)}, u32[]{:S(2)}) copy-start(s32[4096]{0:T(1024)} %copy-done.40) | copy-start | bytes 49156
  610.5 41.4 %copy-start.45 = (f32[2,128]{1,0:T(2,128)S(1)}, f32[2,128]{1,0:T(2,128)}, u32[]{:S(2)}) copy-start(f32[2,128]{1,0:T(2,128)} %copy-done.44) | copy-start | bytes 3076
  651.9 88.4 %copy-start.47 = (f32[2,128]{1,0:T(2,128)S(1)}, f32[2,128]{1,0:T(2,128)}, u32[]{:S(2)}) copy-start(f32[2,128]{1,0:T(2,128)} %get-tuple-element.227) | copy-start | bytes 3076
  (42 other events, 169.0 us)
Sparse Core Ops, SparseCore 0:
  200.6 18.1 reduce-scatter.2
  221.5 77.6 all-gather.1
  553.6 203.0 reduce-scatter.4
